TPU v7x, 32 devices: a whole 2x2x4 slice. The times are simulated.
32 devices in a mesh: dp: 4 (over y, x), sp: 4 (over z), shift: 2 (over core).
Axes of the slice: x: 2, y: 2, z: 4, core: 2. Of those that a mesh axis runs over, the one named last changes fastest.
Arguments:
- query_rows: bfloat16 [8, 1024, 32, 128], P(('shift', 'dp'), 'sp'), parts along dimension 0, may hold values from -6 to 6
- key_rows: bfloat16 [8, 1024, 32, 128], P(('shift', 'dp'), 'sp'), parts along dimension 0, may hold values from -6 to 6
- value_rows: bfloat16 [8, 1024, 32, 128], P(('shift', 'dp'), 'sp'), parts along dimension 0, may hold values from -6 to 6
- out_weight: bfloat16 [8192, 4096], P(('shift', 'dp')), parts along dimension 0, may hold values from -0.09375 to 0.09375
Outputs:
- mixer_out: bfloat16 [8, 1024, 4096], P(('shift', 'dp'), 'sp'), parts along dimension 0
There are 2 independent parts, one for each index of `shift`. A program takes and returns all parts, laid end to end along the dimension named above; each array names one. Nothing has to cross between parts.
All inputs are finite; a program needn't handle non-finite values.
Results may differ from a plain program's by a relative error of at most 0.006.
Values may be sent and summed in bfloat16 or wider, within the bound.
A program may use at most 128 MiB of HBM per device.

v0:
```python
import jax
import jax.numpy as jnp
from jax import lax
from jax.sharding import PartitionSpec as P


def feature_map(values):
    wide = values.astype(jnp.float32)
    return jnp.where(wide > 0.0, wide + 1.0, jnp.exp(jnp.minimum(wide, 0.0))).astype(jnp.bfloat16)


def plain_body(query_rows, key_rows, value_rows, out_weight):
    query_feature, key_feature = (feature_map(query_rows), feature_map(key_rows))
    count = query_rows.shape[1] * lax.axis_size("sp")
    state = (
        jnp.einsum("bthd,bthe->bhde", key_feature, value_rows, preferred_element_type=jnp.float32)
        / count
    )
    mass = jnp.sum(key_feature.astype(jnp.float32), axis=1) / count
    state = lax.psum(state.astype(jnp.bfloat16), "sp")
    mass = lax.psum(mass, "sp")
    top = jnp.einsum("bthd,bhde->bthe", query_feature, state, preferred_element_type=jnp.float32)
    bottom = jnp.einsum(
        "bthd,bhd->bth", query_feature.astype(jnp.float32), mass, precision=lax.Precision.HIGHEST
    )
    mixed = (top / (bottom + 0.001)[..., None] * count**0.5).astype(jnp.bfloat16)
    mixed = mixed.reshape(mixed.shape[0], mixed.shape[1], -1)
    mine = lax.all_to_all(mixed, "dp", split_axis=2, concat_axis=0, tiled=True)
    part = jnp.einsum("btw,wv->btv", mine, out_weight, preferred_element_type=jnp.float32)
    return lax.psum_scatter(part.astype(jnp.bfloat16), "dp", scatter_dimension=0, tiled=True)


def solution(mesh):
    placed = (
        P(("shift", "dp"), "sp", None, None),
        P(("shift", "dp"), "sp", None, None),
        P(("shift", "dp"), "sp", None, None),
        P(("shift", "dp"), None),
    )
    return jax.shard_map(
        plain_body,
        mesh=mesh,
        in_specs=placed,
        out_specs=P(("shift", "dp"), "sp", None),
        check_vma=False,
    )
```

profile of v0, /device:TPU:0, one launch (start us, length us, event | category | flops | bytes accessed | tf_op | source)
XLA Modules:
  0.0 271.4 jit_solution(5975725253797837042)
XLA Ops:
  6.5 0.0 copy-start
  6.5 0.0 all-reduce.3.cloned.1.call-start
  6.5 3.0 %convert_reduce_fusion = (f32[32,128]{1,0:T(8,128)S(1)}, bf16[256,32,128]{2,1,0:T(8,128)(2,1)S(1)}) fusion(bf16[1,256,32,128]{3,2,1,0:T(8,128)(2,1)} %param.5), kind=kLoop, calls=%fused_computation.18 | loop fusion | flops 8384512 | bytes 4210688 | tf_op jit(solution)/shard_map/reduce_sum | solution.py:19
  9.5 0.0 copy-done
  9.5 2.5 multiply_convert_fusion
  12.1 0.0 all-reduce.3.cloned.1.call-update
  12.1 0.0 reduce-scatter.4.cloned.1.call-start
  12.1 4.0 %fusion.13 = bf16[256,32,128]{2,1,0:T(8,128)(2,1)} fusion(bf16[1,256,32,128]{3,2,1,0:T(8,128)(2,1)} %param.4), kind=kLoop, calls=%fused_computation.19 | loop fusion | flops 6291456 | bytes 4194304 | tf_op jit(solution)/shard_map/reshape.5
  16.1 4.3 %copy.16 = bf16[256,32,128]{0,2,1:T(8,128)(2,1)} copy(bf16[256,32,128]{2,1,0:T(8,128)(2,1)} %fusion.13) | data formatting | bytes 4194304 | tf_op jit(solution)/shard_map/reshape.5
  20.4 21.4 %psum.15 = f32[32,128]{1,0:T(8,128)S(1)} all-reduce(f32[32,128]{1,0:T(8,128)S(1)} %broadcast_multiply_fusion), channel_id=1, replica_groups=mesh['dp'=4,'sp'=4,'shift'=2] {'sp'}, use_global_device_ids=true, to_apply=%region_2.3 | all-reduce | flops 4096 | bytes 32768 | tf_op jit(solution)/shard_map/psum | solution.py:21
  41.8 2.5 fusion.24
  44.3 23.1 %all-reduce.3.cloned.1.call-done = bf16[32,128,128]{2,1,0:T(8,128)(2,1)} async-done(((bf16[32,128,128]{2,1,0:T(8,128)(2,1)}), bf16[32,128,128]{2,1,0:T(8,128)(2,1)}) %all-reduce.3.cloned.1.call-update) | async-done | bytes 1048592 | tf_op jit(solution)/shard_map/psum | solution.py:20
  67.4 2.7 fusion.12
  70.1 25.1 %copy.29 = bf16[1,256,4096]{1,0,2:T(2,128)(2,1)} copy(bf16[1,256,4096]{1,2,0:T(8,128)(2,1)S(1)} %bitcast.51) | data formatting | bytes 4194304 | tf_op jit(solution)/shard_map/reshape | solution.py:27
  95.1 0.5 broadcast.38
  95.6 22.9 %reduce.1 = bf16[4096,256]{1,0:T(8,128)(2,1)} reduce(bf16[4096,1,256]{2,1,0:T(2,128)(2,1)} %bitcast.48, bf16[]{:T(256)} %broadcast.38), dimensions={1}, to_apply=%bitcast.46.reduce_sub_computation | reduce | bytes 4194306
  118.5 4.0 %reshape.52 = bf16[4,2,131072]{2,1,0:T(2,128)(2,1)} reshape(bf16[4096,256]{1,0:T(8,128)(2,1)} %reduce.1) | data formatting | bytes 4194304
  122.5 30.2 %all_to_all.18 = bf16[4,2,131072]{2,1,0:T(2,128)(2,1)} all-to-all(bf16[4,2,131072]{2,1,0:T(2,128)(2,1)} %reshape.52), channel_id=1, replica_groups=mesh['dp'=4,'sp'=4,'shift'=2] {'dp'}, dimensions={0} | all-to-all | bytes 4194304 | tf_op jit(solution)/shard_map/all_to_all | solution.py:28
  152.7 5.0 %reshape.53 = bf16[4096,1,256]{2,1,0:T(2,128)(2,1)} reshape(bf16[4,2,131072]{2,1,0:T(2,128)(2,1)} %all_to_all.18) | data formatting | bytes 4194304
  157.7 3.9 %copy.18 = bf16[1,256,4096]{1,2,0:T(8,128)(2,1)} copy(bf16[1,256,4096]{1,0,2:T(2,128)(2,1)} %bitcast.49) | data formatting | bytes 4194304
  161.6 4.0 %copy.13 = bf16[1,256,4,1024]{3,1,2,0:T(8,128)(2,1)} copy(bf16[1,256,4,1024]{1,3,2,0:T(8,128)(2,1)} %bitcast.50) | data formatting | bytes 4194304 | tf_op jit(solution)/shard_map/all_to_all | solution.py:28
  165.5 14.7 %fusion.2 = bf16[4,256,4096]{2,1,0:T(8,128)(2,1)} fusion(bf16[1024,4096]{1,0:T(8,128)(2,1)} %param.7, bf16[1,256,4,1024]{3,1,2,0:T(8,128)(2,1)} %copy.13), kind=kOutput, calls=%fused_computation.2 | convolution fusion | flops 8594128896 | bytes 18874368 | tf_op jit(solution)/shard_map/btw,wv->btv/dot_general | solution.py:29
  180.2 0.0 reduce-scatter.4.cloned.1.call-update
  180.3 84.3 %reduce-scatter.4.cloned.1.call-done = bf16[1,256,4096]{2,1,0:T(8,128)(2,1)} async-done(((bf16[4,256,4096]{2,1,0:T(8,128)(2,1)}), bf16[1,256,4096]{2,1,0:T(8,128)(2,1)}) %reduce-scatter.4.cloned.1.call-update) | async-done | bytes 2097168
  (2 shorter events, 0.0 us)
Async XLA Ops:
  6.5 3.0 %copy-start = (bf16[1,256,32,128]{3,2,1,0:T(8,128)(2,1)S(1)}, bf16[1,256,32,128]{3,2,1,0:T(8,128)(2,1)}, u32[]{:S(2)}) copy-start(bf16[1,256,32,128]{3,2,1,0:T(8,128)(2,1)} %param.6) | copy-start | bytes 6291460
  6.5 60.8 %all-reduce.3.cloned.1.call-start = ((), (), s32[]{:S(2)}) async-start(), calls=%async_computation.2 | async-start | bytes 2097152 | tf_op jit(solution)/shard_map/psum | solution.py:20
  12.1 252.4 %reduce-scatter.4.cloned.1.call-start = ((), (), s32[]{:S(2)}) async-start(), calls=%async_computation.3 | async-start | bytes 10485760
Sparse Core Ops, SparseCore 0:
  12.2 55.1 all-reduce.2
  180.4 84.0 reduce-scatter.3
where the time goes:
time: 272 us; the launch traced here: 271 us
  waiting for transfers between devices  107 us (39%)
  blocking collectives  51.6 us (19%)
  local copies, waits for them, and re-layouts  46.7 us (17%)
  other arithmetic  29.8 us (11%)
  matrix products  22.4 us (8%)
  between operations  13.4 us (5%)
    unnamed x3, waiting for transfers between devices  84.3 us
    all_to_all x1, blocking collectives, plain_body(): mine = lax.all_to_all(mixed, 'dp', split_axis=2, concat_axis=0, tiled=True)  30.2 us
    reshape x1, local copies, waits for them, and re-layouts, plain_body(): mixed = mixed.reshape(mixed.shape[0], mixed.shape[1], -1)  25.1 us
    psum x1, waiting for transfers between devices, plain_body(): state = lax.psum(state.astype(jnp.bfloat16), 'sp')  23.1 us
    unnamed x1, other arithmetic  22.9 us
    psum x1, blocking collectives, plain_body(): mass = lax.psum(mass, 'sp')  21.4 us
    dot_general x1, matrix products, plain_body(): jnp.einsum('btw,wv->btv', mine, out_weight, preferred_element_type=jnp.fl...  14.7 us
    unnamed x6, local copies, waits for them, and re-layouts  13.4 us
  transfers between devices with their start and end apart: 2, of which 2 were waited for; matrix products, arithmetic and copies ran while one was open for 4% of the time, Pallas kernels for 0%

commit v1 on v0

--- a/solution.py
+++ b/solution.py
@@ -25,7 +25,9 @@
     )
     mixed = (top / (bottom + 0.001)[..., None] * count**0.5).astype(jnp.bfloat16)
     mixed = mixed.reshape(mixed.shape[0], mixed.shape[1], -1)
-    mine = lax.all_to_all(mixed, "dp", split_axis=2, concat_axis=0, tiled=True)
+    mine = jnp.concatenate(
+        lax.all_to_all(jnp.stack(jnp.split(mixed, lax.axis_size("dp"), axis=2)), "dp", 0, 0), axis=0
+    )
     part = jnp.einsum("btw,wv->btv", mine, out_weight, preferred_element_type=jnp.float32)
     return lax.psum_scatter(part.astype(jnp.bfloat16), "dp", scatter_dimension=0, tiled=True)
 

time: 272 us -> 214 us (0.79)
  local copies, waits for them, and re-layouts: 46.7 us -> 11.8 us
  other arithmetic: 29.8 us -> 8.58 us
    reshape x1 -> x0, local copies, waits for them, and re-layouts: 25.1 us -> none  [plain_body(): mixed = mixed.reshape(mixed.shape[0], mixed.shape[1], -1)]
    unnamed x1 -> x0, other arithmetic: 22.9 us -> none
    unnamed x6, local copies, waits for them, and re-layouts: 13.4 us -> 6.37 us
    all_to_all x1 -> x0, local copies, waits for them, and re-layouts: 3.97 us -> none  [plain_body(): mine = lax.all_to_all(mixed, 'dp', split_axis=2, concat_axis=0, tiled=True)]
    another operation x1 -> x2, other arithmetic: 4 us -> 5.61 us
  transfers between devices with their start and end apart: 2 -> 2, of which waited for: 2 -> 2; matrix products, arithmetic and copies ran while one was open for 4% -> 5% of each run, Pallas kernels for 0% -> 0%
where the time goes in v1:
time: 214 us
  waiting for transfers between devices  107 us (50%)
  blocking collectives  50.3 us (24%)
  matrix products  22 us (10%)
  between operations  13.4 us (6%)
  local copies, waits for them, and re-layouts  11.8 us (6%)
  other arithmetic  8.58 us (4%)
    unnamed x3, waiting for transfers between devices  84.3 us
    all_to_all x1, blocking collectives, plain_body(): lax.all_to_all(jnp.stack(jnp.split(mixed, lax.axis_size('dp'), axis=2)),...  28.9 us
    psum x1, waiting for transfers between devices, plain_body(): state = lax.psum(state.astype(jnp.bfloat16), 'sp')  23.1 us
    psum x1, blocking collectives, plain_body(): mass = lax.psum(mass, 'sp')  21.4 us
    dot_general x1, matrix products, plain_body(): jnp.einsum('btw,wv->btv', mine, out_weight, preferred_element_type=jnp.fl...  14.3 us
    unnamed x6, local copies, waits for them, and re-layouts  6.37 us
  transfers between devices with their start and end apart: 2, of which 2 were waited for; matrix products, arithmetic and copies ran while one was open for 5% of the time, Pallas kernels for 0%

profile of v1, /device:TPU:0, one launch (start us, length us, event | category | flops | bytes accessed | tf_op | source)
XLA Modules:
  0.0 213.5 jit_solution(17224997726878175967)
XLA Ops:
  6.5 0.0 copy-start
  6.5 0.0 all-reduce.3.cloned.1.call-start
  6.5 3.0 %convert_reduce_fusion = (f32[32,128]{1,0:T(8,128)S(1)}, bf16[256,32,128]{2,1,0:T(8,128)(2,1)S(1)}) fusion(bf16[1,256,32,128]{3,2,1,0:T(8,128)(2,1)} %param.5), kind=kLoop, calls=%fused_computation.18 | loop fusion | flops 8384512 | bytes 4210688 | tf_op jit(solution)/shard_map/reduce_sum | solution.py:19
  9.5 0.0 copy-done
  9.5 2.5 %multiply_convert_fusion = bf16[32,128,128]{1,2,0:T(8,128)(2,1)} fusion(bf16[256,32,128]{2,1,0:T(8,128)(2,1)S(1)} %bitcast.44, bf16[256,32,128]{2,1,0:T(8,128)(2,1)S(1)} %get-tuple-element.10), kind=kOutput, calls=%fused_computation.25 | convolution fusion | flops 269484032 | bytes 5242880 | tf_op jit(solution)/shard_map/bthd,bthe->bhde/dot_general | solution.py:16
  12.1 0.0 all-reduce.3.cloned.1.call-update
  12.1 0.0 reduce-scatter.4.cloned.1.call-start
  12.1 4.0 %fusion.13 = bf16[256,32,128]{2,1,0:T(8,128)(2,1)} fusion(bf16[1,256,32,128]{3,2,1,0:T(8,128)(2,1)} %param.4), kind=kLoop, calls=%fused_computation.19 | loop fusion | flops 6291456 | bytes 4194304 | tf_op jit(solution)/shard_map/reshape.6
  16.1 4.3 %copy.18 = bf16[256,32,128]{0,2,1:T(8,128)(2,1)} copy(bf16[256,32,128]{2,1,0:T(8,128)(2,1)} %fusion.13) | data formatting | bytes 4194304 | tf_op jit(solution)/shard_map/reshape.6
  20.4 21.4 %psum.15 = f32[32,128]{1,0:T(8,128)S(1)} all-reduce(f32[32,128]{1,0:T(8,128)S(1)} %broadcast_multiply_fusion), channel_id=1, replica_groups=mesh['dp'=4,'sp'=4,'shift'=2] {'sp'}, use_global_device_ids=true, to_apply=%region_2.3 | all-reduce | flops 4096 | bytes 32768 | tf_op jit(solution)/shard_map/psum | solution.py:21
  41.8 2.5 %fusion.25 = f32[32,1,256]{2,1,0:T(1,128)S(1)} fusion(f32[32,128,1]{1,2,0:T(1,128)S(1)} %bitcast.50, bf16[256,32,128]{0,2,1:T(8,128)(2,1)} %copy.18), kind=kOutput, calls=%fused_computation.31 | convolution fusion | flops 12582912 | bytes 2146304 | tf_op jit(solution)/shard_map/bthd,bhd->bth/dot_general | solution.py:23
  44.3 23.1 %all-reduce.3.cloned.1.call-done = bf16[32,128,128]{1,2,0:T(8,128)(2,1)} async-done(((bf16[32,128,128]{1,2,0:T(8,128)(2,1)}), bf16[32,128,128]{1,2,0:T(8,128)(2,1)}) %all-reduce.3.cloned.1.call-update) | async-done | bytes 1048592 | tf_op jit(solution)/shard_map/psum | solution.py:20
  67.4 2.6 %fusion.12 = bf16[1,256,32,128]{1,3,2,0:T(8,128)(2,1)S(1)} fusion(bf16[32,128,128]{1,2,0:T(8,128)(2,1)} %all-reduce.3.cloned.1.call-done, bf16[256,32,128]{0,2,1:T(8,128)(2,1)} %copy.18, f32[256,32]{0,1:T(8,128)S(1)} %fusion.23), kind=kOutput, calls=%fused_computation.17 | convolution fusion | flops 271581184 | bytes 5275648 | tf_op jit(solution)/shard_map/bthd,bhde->bthe/dot_general | solution.py:22
  70.0 1.2 fusion.24
  71.2 1.2 copy.20
  72.4 2.1 copy.22
  74.5 2.1 copy.21
  76.5 1.0 copy.23
  77.5 1.6 pad_maximum_fusion
  79.2 28.9 %all_to_all.5 = bf16[4,1,256,1024]{3,2,1,0:T(8,128)(2,1)S(1)} all-to-all(bf16[4,1,256,1024]{3,2,1,0:T(8,128)(2,1)S(1)} %pad_maximum_fusion), channel_id=1, replica_groups=mesh['dp'=4,'sp'=4,'shift'=2] {'dp'}, dimensions={0} | all-to-all | bytes 4194304 | tf_op jit(solution)/shard_map/all_to_all | solution.py:29
  108.1 14.3 %fusion.2 = bf16[4,256,4096]{2,1,0:T(8,128)(2,1)} fusion(bf16[1024,4096]{1,0:T(8,128)(2,1)} %param.7, bf16[4,1,256,1024]{3,2,1,0:T(8,128)(2,1)S(1)} %all_to_all.5), kind=kOutput, calls=%fused_computation.2 | convolution fusion | flops 8594128896 | bytes 18874368 | tf_op jit(solution)/shard_map/btw,wv->btv/dot_general | solution.py:31
  122.4 0.0 reduce-scatter.4.cloned.1.call-update
  122.5 84.2 %reduce-scatter.4.cloned.1.call-done = bf16[1,256,4096]{2,1,0:T(8,128)(2,1)} async-done(((bf16[4,256,4096]{2,1,0:T(8,128)(2,1)}), bf16[1,256,4096]{2,1,0:T(8,128)(2,1)}) %reduce-scatter.4.cloned.1.call-update) | async-done | bytes 2097168
  (2 shorter events, 0.0 us)
Async XLA Ops:
  6.5 3.0 %copy-start = (bf16[1,256,32,128]{3,2,1,0:T(8,128)(2,1)S(1)}, bf16[1,256,32,128]{3,2,1,0:T(8,128)(2,1)}, u32[]{:S(2)}) copy-start(bf16[1,256,32,128]{3,2,1,0:T(8,128)(2,1)} %param.6) | copy-start | bytes 6291460
  6.5 60.8 %all-reduce.3.cloned.1.call-start = ((), (), s32[]{:S(2)}) async-start(), calls=%async_computation.2 | async-start | bytes 2097152 | tf_op jit(solution)/shard_map/psum | solution.py:20
  12.1 194.6 %reduce-scatter.4.cloned.1.call-start = ((), (), s32[]{:S(2)}) async-start(), calls=%async_computation.3 | async-start | bytes 10485760
Sparse Core Ops, SparseCore 0:
  12.2 55.1 all-reduce.2
  122.6 84.0 reduce-scatter.3
